TPU v7x, 32 devices: a whole 2x2x4 slice. The times are simulated.
32 devices in a mesh: dp: 8 (over z, core), ctx: 4 (over y, x).
Axes of the slice: x: 2, y: 2, z: 4, core: 2. Of those that a mesh axis runs over, the one named last changes fastest.
Arguments:
- qkv: bfloat16 [8, 512, 5120], P('dp', 'ctx'), may hold values from -8 to 8
- dest: int32 [8, 8], P('dp'), may hold values from 0 to 7, as said below
- order: int32 [8], replicated, may hold values from 0 to 7, as said below
- lengths: int32 [8, 8], replicated, may hold values from 1 to 256, 512 in all within a row
Outputs:
- attended: bfloat16 [8, 512, 4096], P('dp', 'ctx')
Inputs may be any that keep to these rules, and one draw needn't show every extreme that they name: `dest`: entry [r, s] is r itself, r + 1 or r - 1 (indices modulo 8), and the relation is mutual: if entry [r, s] is t, entry [t, s] is r. For every c below 4: order[2 c] is below 4 and order[2 c + 1] = 7 - order[2 c]; every span appears once.
All inputs are finite; a program needn't handle non-finite values.
Results may differ from a plain program's by a relative error of at most 0.0031.
Values may be sent and summed in bfloat16 or wider, within the bound.
A program may use at most 64 MiB of HBM per device.

v0:
```python
import math
import jax
import jax.numpy as jnp
from jax import lax
from jax.sharding import PartitionSpec as P

QUERY_HEADS = 32
KEY_VALUE_HEADS = 4
HEAD_SIZE = 128
NDOC = 8
QUERIES_PER_KV = 8
MASK_FLOOR = -1e30


def passed_along(array, axis, by):
    devices = lax.axis_size(axis)
    return lax.ppermute(array, axis, [(i, (i + by) % devices) for i in range(devices)])


def slot_layout(order, sources, doc_ends, exchanged_rows):
    slot_count = order.shape[0]
    offsets = jnp.arange(exchanged_rows, dtype=jnp.int32)
    positions = (order[:, None] * exchanged_rows + offsets[None, :]).reshape(
        slot_count * exchanged_rows
    )
    slot_ends = jnp.take(doc_ends, sources, axis=0)
    row_ends = jnp.repeat(slot_ends, exchanged_rows, axis=0)
    counted = jnp.sum((row_ends <= positions[:, None]).astype(jnp.int32), axis=1)
    row_source = jnp.repeat(sources, exchanged_rows)
    documents = row_source * NDOC + counted
    return (positions, documents)


def attend(carried, query_head_rows, key_rows, value_rows, visible):
    running_max, accumulated_sum, weighted_values = carried
    scores = jnp.einsum(
        "hqd,khd->hqk", query_head_rows, key_rows, preferred_element_type=jnp.float32
    ) * (1.0 / math.sqrt(HEAD_SIZE))
    tiled_mask = jnp.tile(visible, (QUERIES_PER_KV, 1))[None]
    scores = jnp.where(tiled_mask, scores, MASK_FLOOR)
    new_max = jnp.maximum(running_max, jnp.max(scores, axis=2, keepdims=True))
    weights = jnp.where(tiled_mask, jnp.exp(scores - new_max), 0.0)
    rescale = jnp.exp(running_max - new_max)
    accumulated_sum = accumulated_sum * rescale + jnp.sum(weights, axis=2, keepdims=True)
    update = jnp.einsum(
        "hqk,khd->hqd", weights.astype(jnp.bfloat16), value_rows, preferred_element_type=jnp.float32
    )
    return (new_max, accumulated_sum, weighted_values * rescale + update)


def keep_state(carried, query_head_rows, key_rows, value_rows, visible):
    return carried


def on_device(qkv, dest, order, lengths):
    dp_index = lax.axis_index("dp")
    dp_count = lax.axis_size("dp")
    ctx_index = lax.axis_index("ctx")
    local_rows = qkv.shape[1]
    exchanged_rows = local_rows // 2
    query_width = QUERY_HEADS * HEAD_SIZE
    below = (dp_index + dp_count - 1) % dp_count
    above = (dp_index + 1) % dp_count
    sources = dest[0]
    doc_ends = jnp.cumsum(lengths, axis=1)
    positions, documents = slot_layout(order, sources, doc_ends, exchanged_rows)
    own_sources = lax.dynamic_slice_in_dim(sources, 2 * ctx_index, 2)
    row_from = jnp.repeat(own_sources, exchanged_rows)[:, None]
    resident = qkv[0]
    from_below = passed_along(resident, "dp", 1)
    from_above = passed_along(resident, "dp", -1)
    settled = jnp.where(
        row_from == below, from_below, jnp.where(row_from == above, from_above, resident)
    )
    query_rows = settled[:, :query_width]
    key_values = settled[:, query_width:]
    own_positions = lax.dynamic_slice_in_dim(positions, ctx_index * local_rows, local_rows).reshape(
        2, exchanged_rows
    )
    own_documents = lax.dynamic_slice_in_dim(documents, ctx_index * local_rows, local_rows).reshape(
        2, exchanged_rows
    )
    query_head_rows = query_rows.reshape(
        2, exchanged_rows, KEY_VALUE_HEADS, QUERIES_PER_KV, HEAD_SIZE
    )
    query_head_rows = jnp.transpose(query_head_rows, (0, 2, 3, 1, 4)).reshape(
        2, KEY_VALUE_HEADS, QUERIES_PER_KV * exchanged_rows, HEAD_SIZE
    )

    def fresh_state():
        return (
            jnp.full(
                (KEY_VALUE_HEADS, QUERIES_PER_KV * exchanged_rows, 1), MASK_FLOOR, jnp.float32
            ),
            jnp.zeros((KEY_VALUE_HEADS, QUERIES_PER_KV * exchanged_rows, 1), jnp.float32),
            jnp.zeros((KEY_VALUE_HEADS, QUERIES_PER_KV * exchanged_rows, HEAD_SIZE), jnp.float32),
        )

    portion = lax.all_gather(key_values, "ctx", axis=0, tiled=True)
    piece_rows = portion.shape[0]
    count_of_blocks = piece_rows // local_rows
    block_list = portion.reshape(count_of_blocks, local_rows, 2, KEY_VALUE_HEADS, HEAD_SIZE)

    def absorb_block(states, inputs):
        block_pairs, block_index = inputs
        first_row = block_index * local_rows
        key_positions = lax.dynamic_slice_in_dim(positions, first_row, local_rows)
        key_documents = lax.dynamic_slice_in_dim(documents, first_row, local_rows)
        key_rows = block_pairs[:, 0]
        value_rows = block_pairs[:, 1]
        updated = []
        for half_index in range(2):
            visible = (key_documents[None, :] == own_documents[half_index][:, None]) & (
                key_positions[None, :] <= own_positions[half_index][:, None]
            )
            updated.append(
                lax.cond(
                    jnp.any(visible),
                    attend,
                    keep_state,
                    states[half_index],
                    query_head_rows[half_index],
                    key_rows,
                    value_rows,
                    visible,
                )
            )
        return ((updated[0], updated[1]), None)

    result, unused = lax.scan(
        absorb_block,
        (fresh_state(), fresh_state()),
        (block_list, jnp.arange(count_of_blocks, dtype=jnp.int32)),
    )
    finished = []
    for half_index in range(2):
        running_max, accumulated_sum, weighted_values = result[half_index]
        normalized_output = (weighted_values / accumulated_sum).reshape(
            KEY_VALUE_HEADS, QUERIES_PER_KV, exchanged_rows, HEAD_SIZE
        )
        finished.append(
            jnp.transpose(normalized_output, (2, 0, 1, 3)).reshape(
                exchanged_rows, QUERY_HEADS * HEAD_SIZE
            )
        )
    attended = jnp.concatenate(finished, axis=0).astype(jnp.bfloat16)
    return attended[None]


def solution(mesh):
    return jax.shard_map(
        on_device,
        mesh=mesh,
        in_specs=(P("dp", "ctx", None), P("dp", None), P(), P()),
        out_specs=P("dp", "ctx", None),
        check_vma=False,
    )
```

profile of v0, /device:TPU:1, one launch (start us, length us, event | category | flops | bytes accessed | tf_op | source)
XLA Modules:
  0.0 125.5 jit_solution(16273775453789031055)
XLA Ops:
  6.5 2.7 %collective-permute-start = (bf16[128,5120]{1,0:T(8,128)(2,1)}, bf16[128,5120]{1,0:T(8,128)(2,1)S(1)}, u32[]{:S(2)}, u32[]{:S(2)}) collective-permute-start(bf16[128,5120]{1,0:T(8,128)(2,1)} %bitcast.102), channel_id=1, source_target_pairs={{0,4},{4,8},{8,12},{12,16},{16,20},{20,24},{24,28},{28,0},{1,5},{5... | collective-permute-start | bytes 3932168 | tf_op jit(solution)/shard_map/ppermute | solution.py:17
  9.2 0.7 compare_bitcast_fusion.1
  10.3 0.8 reduce_window_sum.11
  12.5 23.6 %collective-permute-done = bf16[128,5120]{1,0:T(8,128)(2,1)S(1)} collective-permute-done((bf16[128,5120]{1,0:T(8,128)(2,1)}, bf16[128,5120]{1,0:T(8,128)(2,1)S(1)}, u32[]{:S(2)}, u32[]{:S(2)}) %collective-permute-start) | collective-permute-done | bytes 1310752 | tf_op jit(solution)/shard_map/ppermute | solution.py:17
  36.1 4.0 %collective-permute-done.1 = bf16[128,5120]{1,0:T(8,128)(2,1)} collective-permute-done((bf16[128,5120]{1,0:T(8,128)(2,1)}, bf16[128,5120]{1,0:T(8,128)(2,1)}, u32[]{:S(2)}, u32[]{:S(2)}) %collective-permute-start.1) | collective-permute-done | bytes 1310752 | tf_op jit(solution)/shard_map/ppermute | solution.py:17
  40.0 2.0 %select_select_fusion = bf16[128,5120]{1,0:T(8,128)(2,1)S(1)} fusion(bf16[128,5120]{1,0:T(8,128)(2,1)S(1)} %collective-permute-done, bf16[128,5120]{1,0:T(8,128)(2,1)} %collective-permute-done.1, pred[128]{0:T(512)(128)(4,1)S(1)} %eq.74, pred[128]{0:T(512)(128)(4,1)S(1)} %eq.70, bf16[1,128,5120]{2,1,0:T(8,128)(2,1)} %param.10), kind=kLoop, calls=%fused_computation.43 | loop fusion | flops 1310720 | bytes 5243136 | tf_op jit(solution)/shard_map/jit(_where)/select_n | solution.py:72
  42.0 0.7 slice.38
  44.3 0.7 dynamic_slice.23
  45.7 0.7 dynamic_slice.24
  47.4 1.4 %copy.22 = bf16[2,64,4,8,128]{4,1,3,2,0:T(8,128)(2,1)} copy(bf16[2,64,4,8,128]{4,3,2,1,0:T(8,128)(2,1)S(1)} %bitcast.97) | data formatting | bytes 2097152 | tf_op jit(solution)/shard_map/reshape | solution.py:83
  48.8 20.3 %all-gather.2.cloned.1.call-done = bf16[512,1024]{1,0:T(8,128)(2,1)} async-done(((bf16[128,1024]{1,0:T(8,128)(2,1)}), bf16[512,1024]{1,0:T(8,128)(2,1)}) %all-gather.2.cloned.1.call-update) | async-done | bytes 1048592 | tf_op jit(solution)/shard_map/all_gather | solution.py:99
  69.1 1.8 %reshape.165 = bf16[4,128,2,4,128]{4,3,2,1,0:T(4,128)(2,1)S(1)} reshape(bf16[512,1024]{1,0:T(8,128)(2,1)} %all-gather.2.cloned.1.call-done) | data formatting | bytes 2097152 | tf_op jit(solution)/shard_map/reshape | solution.py:102
  72.8 42.2 %while.20 = (s32[]{:T(128)}, f32[4,512,1]{1,0,2:T(4,128)S(1)}, f32[4,512,1]{1,0,2:T(4,128)}, f32[4,512,128]{2,1,0:T(8,128)S(1)}, f32[4,512,1]{1,0,2:T(4,128)S(1)...) while((s32[]{:T(128)}, f32[4,512,1]{1,0,2:T(4,128)S(1)}, ...), condition=%wide.region_13.14_spmd, body=%wide.region_2.13_spmd.sunk | while | flops 274280448 | bytes 14785039 | solution.py:130
  72.8 1.2 dynamic_slice.37
  74.6 0.7 dynamic_slice.38
  75.3 0.7 dynamic_slice.39
  76.1 0.7 slice_bitcast_fusion.9
  76.8 1.4 %fusion.32 = (pred[]{:T(512)}, pred[64,128]{1,0:T(8,128)(4,1)S(1)}, pred[]{:T(512)}, pred[64,128]{1,0:T(8,128)(4,1)}) fusion(s32[64]{0:T(128)S(1)} %get-tuple-element.331, s32[128]{0:T(128)S(1)} %dynamic_slice.38, s32[64]{0:T(128)S(1)} %get-tuple-element.332, s32[128]{0:T(128)S(1)} %dynamic_slice.39, s32[64]{0:T(128)S(1)} %get-tuple-element.333, ...), kind=kLoop, calls=%fused_computation.64.clone.1 | loop fusion | flops 65534 | bytes 18434 | tf_op jit(solution)/shard_map/while/body/eval_jaxpr/reduce_or | solution.py:118
  79.1 3.9 %conditional.5 = ((f32[4,512,1]{1,0,2:T(4,128)S(1)}, f32[4,512,1]{1,0,2:T(4,128)}, f32[4,512,128]{2,1,0:T(8,128)S(1)})) conditional(s32[]{:T(128)} %convert_element_type.33, (f32[4,512,1]{1,0,2:T(4,128)S(1)}, f32[4,512,1]{1,0,2:T(4,128)}, f32[4,512,128]{2,1,0:T(8,128)S(1)}) %tuple.61, (pred[64,128]{1,0:T(8,128)(4,1)S(1)}, ...), branch_computations={%region_9.9_spmd, %region_10.12_spmd} | conditional | flops 137107456 | bytes 6561824 | solution.py:117
  79.3 1.4 %fusion.26 = (f32[4,512]{1,0:T(4,128)S(1)}, f32[4,512,128]{1,2,0:T(8,128)S(1)}) fusion(bf16[128,4,128]{2,0,1:T(8,128)(2,1)S(1)} %get-tuple-element.115, bf16[2,4,512,128]{3,2,1,0:T(8,128)(2,1)} %get-tuple-element.114, pred[512,128]{0,1:T(8,128)(4,1)S(1)} %copy.20), kind=kOutput, calls=%fused_computation.67 | convolution fusion | flops 67893248 | bytes 1777664 | tf_op jit(solution)/shard_map/while/body/eval_jaxpr/cond/branch_1_fun/hqd,khd->hqk/dot_general | solution.py:36
  80.9 1.3 %bitcast_add_fusion.1 = f32[4,512,1]{1,0,2:T(4,128)} fusion(f32[4,512]{1,0:T(4,128)S(1)} %fusion.13, f32[4,512,1]{1,0,2:T(4,128)} %get-tuple-element.116, f32[4,512,1]{1,0,2:T(4,128)S(1)} %get-tuple-element.112, f32[4,512,1]{1,0,2:T(4,128)S(1)} %get-tuple-element.356), kind=kLoop, calls=%fused_computation.28 | loop fusion | flops 6144 | bytes 40960 | tf_op jit(solution)/shard_map/while/body/eval_jaxpr/cond/branch_1_fun/add | solution.py:44
  83.6 3.3 %conditional.4 = ((f32[4,512,1]{1,0,2:T(4,128)S(1)}, f32[4,512,1]{1,0,2:T(4,128)}, f32[4,512,128]{2,1,0:T(8,128)S(1)})) conditional(s32[]{:T(128)} %convert_element_type.32, (f32[4,512,1]{1,0,2:T(4,128)S(1)}, f32[4,512,1]{1,0,2:T(4,128)}, f32[4,512,128]{2,1,0:T(8,128)S(1)}) %tuple.59, (pred[64,128]{1,0:T(8,128)(4,1)}, ...), branch_computations={%region_4.4_spmd, %region_5.7_spmd} | conditional | flops 137107456 | bytes 6627416 | solution.py:117
  84.5 1.4 %fusion.25 = (f32[4,512]{1,0:T(4,128)S(1)}, f32[4,512,128]{1,2,0:T(8,128)S(1)}) fusion(bf16[128,4,128]{2,0,1:T(8,128)(2,1)S(1)} %get-tuple-element.108, bf16[2,4,512,128]{3,2,1,0:T(8,128)(2,1)} %get-tuple-element.107, pred[512,128]{0,1:T(8,128)(4,1)S(1)} %copy.18), kind=kOutput, calls=%fused_computation.66 | convolution fusion | flops 67893248 | bytes 1777664 | tf_op jit(solution)/shard_map/while/body/eval_jaxpr/cond/branch_1_fun/hqd,khd->hqk/dot_general | solution.py:36
  86.1 0.7 convolution_add_fusion
  86.9 1.2 dynamic_slice.37
  88.7 0.7 dynamic_slice.38
  89.5 0.7 dynamic_slice.39
  90.2 0.7 slice_bitcast_fusion.9
  91.0 1.4 %fusion.32 = (pred[]{:T(512)}, pred[64,128]{1,0:T(8,128)(4,1)S(1)}, pred[]{:T(512)}, pred[64,128]{1,0:T(8,128)(4,1)}) fusion(s32[64]{0:T(128)S(1)} %get-tuple-element.331, s32[128]{0:T(128)S(1)} %dynamic_slice.38, s32[64]{0:T(128)S(1)} %get-tuple-element.332, s32[128]{0:T(128)S(1)} %dynamic_slice.39, s32[64]{0:T(128)S(1)} %get-tuple-element.333, ...), kind=kLoop, calls=%fused_computation.64.clone.1 | loop fusion | flops 65534 | bytes 18434 | tf_op jit(solution)/shard_map/while/body/eval_jaxpr/reduce_or | solution.py:118
  93.9 3.3 %conditional.4 = ((f32[4,512,1]{1,0,2:T(4,128)S(1)}, f32[4,512,1]{1,0,2:T(4,128)}, f32[4,512,128]{2,1,0:T(8,128)S(1)})) conditional(s32[]{:T(128)} %convert_element_type.32, (f32[4,512,1]{1,0,2:T(4,128)S(1)}, f32[4,512,1]{1,0,2:T(4,128)}, f32[4,512,128]{2,1,0:T(8,128)S(1)}) %tuple.59, (pred[64,128]{1,0:T(8,128)(4,1)}, ...), branch_computations={%region_4.4_spmd, %region_5.7_spmd} | conditional | flops 137107456 | bytes 6627416 | solution.py:117
  93.9 0.7 tile.4
  94.8 1.4 %fusion.25 = (f32[4,512]{1,0:T(4,128)S(1)}, f32[4,512,128]{1,2,0:T(8,128)S(1)}) fusion(bf16[128,4,128]{2,0,1:T(8,128)(2,1)S(1)} %get-tuple-element.108, bf16[2,4,512,128]{3,2,1,0:T(8,128)(2,1)} %get-tuple-element.107, pred[512,128]{0,1:T(8,128)(4,1)S(1)} %copy.18), kind=kOutput, calls=%fused_computation.66 | convolution fusion | flops 67893248 | bytes 1777664 | tf_op jit(solution)/shard_map/while/body/eval_jaxpr/cond/branch_1_fun/hqd,khd->hqk/dot_general | solution.py:36
  96.4 0.7 convolution_add_fusion
  97.2 1.2 dynamic_slice.37
  99.0 0.7 dynamic_slice.38
  99.8 0.7 dynamic_slice.39
  100.5 0.7 slice_bitcast_fusion.9
  101.2 1.4 %fusion.32 = (pred[]{:T(512)}, pred[64,128]{1,0:T(8,128)(4,1)S(1)}, pred[]{:T(512)}, pred[64,128]{1,0:T(8,128)(4,1)}) fusion(s32[64]{0:T(128)S(1)} %get-tuple-element.331, s32[128]{0:T(128)S(1)} %dynamic_slice.38, s32[64]{0:T(128)S(1)} %get-tuple-element.332, s32[128]{0:T(128)S(1)} %dynamic_slice.39, s32[64]{0:T(128)S(1)} %get-tuple-element.333, ...), kind=kLoop, calls=%fused_computation.64.clone.1 | loop fusion | flops 65534 | bytes 18434 | tf_op jit(solution)/shard_map/while/body/eval_jaxpr/reduce_or | solution.py:118
  103.5 3.9 %conditional.5 = ((f32[4,512,1]{1,0,2:T(4,128)S(1)}, f32[4,512,1]{1,0,2:T(4,128)}, f32[4,512,128]{2,1,0:T(8,128)S(1)})) conditional(s32[]{:T(128)} %convert_element_type.33, (f32[4,512,1]{1,0,2:T(4,128)S(1)}, f32[4,512,1]{1,0,2:T(4,128)}, f32[4,512,128]{2,1,0:T(8,128)S(1)}) %tuple.61, (pred[64,128]{1,0:T(8,128)(4,1)S(1)}, ...), branch_computations={%region_9.9_spmd, %region_10.12_spmd} | conditional | flops 137107456 | bytes 6561824 | solution.py:117
  103.7 1.4 %fusion.26 = (f32[4,512]{1,0:T(4,128)S(1)}, f32[4,512,128]{1,2,0:T(8,128)S(1)}) fusion(bf16[128,4,128]{2,0,1:T(8,128)(2,1)S(1)} %get-tuple-element.115, bf16[2,4,512,128]{3,2,1,0:T(8,128)(2,1)} %get-tuple-element.114, pred[512,128]{0,1:T(8,128)(4,1)S(1)} %copy.20), kind=kOutput, calls=%fused_computation.67 | convolution fusion | flops 67893248 | bytes 1777664 | tf_op jit(solution)/shard_map/while/body/eval_jaxpr/cond/branch_1_fun/hqd,khd->hqk/dot_general | solution.py:36
  105.3 1.3 %bitcast_add_fusion.1 = f32[4,512,1]{1,0,2:T(4,128)} fusion(f32[4,512]{1,0:T(4,128)S(1)} %fusion.13, f32[4,512,1]{1,0,2:T(4,128)} %get-tuple-element.116, f32[4,512,1]{1,0,2:T(4,128)S(1)} %get-tuple-element.112, f32[4,512,1]{1,0,2:T(4,128)S(1)} %get-tuple-element.356), kind=kLoop, calls=%fused_computation.28 | loop fusion | flops 6144 | bytes 40960 | tf_op jit(solution)/shard_map/while/body/eval_jaxpr/cond/branch_1_fun/add | solution.py:44
  108.0 1.2 dynamic_slice.37
  109.8 0.7 dynamic_slice.38
  110.6 0.7 dynamic_slice.39
  111.3 0.7 slice_bitcast_fusion.9
  112.1 1.4 %fusion.32 = (pred[]{:T(512)}, pred[64,128]{1,0:T(8,128)(4,1)S(1)}, pred[]{:T(512)}, pred[64,128]{1,0:T(8,128)(4,1)}) fusion(s32[64]{0:T(128)S(1)} %get-tuple-element.331, s32[128]{0:T(128)S(1)} %dynamic_slice.38, s32[64]{0:T(128)S(1)} %get-tuple-element.332, s32[128]{0:T(128)S(1)} %dynamic_slice.39, s32[64]{0:T(128)S(1)} %get-tuple-element.333, ...), kind=kLoop, calls=%fused_computation.64.clone.1 | loop fusion | flops 65534 | bytes 18434 | tf_op jit(solution)/shard_map/while/body/eval_jaxpr/reduce_or | solution.py:118
  115.0 1.4 %divide_convert_fusion = (bf16[4,512,128]{2,1,0:T(8,128)(2,1)S(1)}, bf16[4,512,128]{2,1,0:T(8,128)(2,1)S(1)}) fusion(f32[4,512,128]{2,1,0:T(8,128)S(1)} %get-tuple-element.146, f32[4,512]{1,0:T(4,128)} %bitcast.31, f32[4,512,128]{2,1,0:T(8,128)S(1)} %get-tuple-element.144, f32[4,512]{1,0:T(4,128)} %bitcast.105), kind=kLoop, calls=%fused_computation.46 | loop fusion | flops 1048576 | bytes 3162112 | tf_op jit(solution)/shard_map/convert.4
  117.6 1.0 pad_maximum_fusion
  (83 shorter events, 12.3 us)
Async XLA Ops:
  6.5 62.6 %all-gather.2.cloned.1.call-start = ((), (), s32[]{:S(2)}) async-start(), calls=%async_computation | async-start | bytes 1310720 | tf_op jit(solution)/shard_map/all_gather | solution.py:99
  6.5 29.5 %collective-permute-start = (bf16[128,5120]{1,0:T(8,128)(2,1)}, bf16[128,5120]{1,0:T(8,128)(2,1)S(1)}, u32[]{:S(2)}, u32[]{:S(2)}) collective-permute-start(bf16[128,5120]{1,0:T(8,128)(2,1)} %bitcast.102), channel_id=1, source_target_pairs={{0,4},{4,8},{8,12},{12,16},{16,20},{20,24},{24,28},{28,0},{1,5},{5... | collective-permute-start | bytes 3932168 | tf_op jit(solution)/shard_map/ppermute | solution.py:17
  9.2 30.8 %collective-permute-start.1 = (bf16[128,5120]{1,0:T(8,128)(2,1)}, bf16[128,5120]{1,0:T(8,128)(2,1)}, u32[]{:S(2)}, u32[]{:S(2)}) collective-permute-start(bf16[128,5120]{1,0:T(8,128)(2,1)} %bitcast.103), channel_id=1, source_target_pairs={{0,28},{4,0},{8,4},{12,8},{16,12},{20,16},{24,20},{28,24},{1,29},{... | collective-permute-start | bytes 3932168 | tf_op jit(solution)/shard_map/ppermute | solution.py:17
  12.5 30.2 %copy-start.2 = (s32[1,8]{1,0:T(1,128)S(1)}, s32[1,8]{1,0:T(1,128)}, u32[]{:S(2)}) copy-start(s32[1,8]{1,0:T(1,128)} %param.11) | copy-start | bytes 100
  84.5 1.6 %copy-start = (f32[4,512,1]{1,0,2:T(4,128)S(1)}, f32[4,512,1]{1,0,2:T(4,128)}, u32[]{:S(2)}) copy-start(f32[4,512,1]{1,0,2:T(4,128)} %get-tuple-element.109) | copy-start | bytes 24580 | tf_op jit(solution)/shard_map/while/body/eval_jaxpr/cond
  86.1 0.7 copy-start.1
  94.8 1.6 %copy-start = (f32[4,512,1]{1,0,2:T(4,128)S(1)}, f32[4,512,1]{1,0,2:T(4,128)}, u32[]{:S(2)}) copy-start(f32[4,512,1]{1,0,2:T(4,128)} %get-tuple-element.109) | copy-start | bytes 24580 | tf_op jit(solution)/shard_map/while/body/eval_jaxpr/cond
  96.4 0.7 copy-start.1
Sparse Core Ops, SparseCore 0:
  42.9 26.1 all-gather.1
where the time goes:
time: 126 us; the launch traced here: 125 us
  waiting for transfers between devices  47.9 us (38%)
  local copies, waits for them, and re-layouts  28.8 us (23%)
  other arithmetic  16.2 us (13%)
  between operations  13.5 us (11%)
  matrix products  8.41 us (7%)
  loops' own time  8.04 us (6%)
  starting transfers between devices  2.68 us (2%)
    ppermute x2, waiting for transfers between devices, passed_along(): lax.ppermute(array, axis, [(i, (i + by) % devices) for i in range(devices)])  27.5 us
    all_gather x1, waiting for transfers between devices, on_device(): portion = lax.all_gather(key_values, 'ctx', axis=0, tiled=True)  20.3 us
    another operation x1, loops' own time, on_device(): lax.scan(absorb_block, (fresh_state(), fresh_state()), (block_list, jnp.a...  7.71 us
    reduce_or x4, other arithmetic, absorb_block(): jnp.any(visible)  5.6 us
    dot_general x4, matrix products, attend(): jnp.einsum('hqd,khd->hqk', query_head_rows, key_rows, preferred_element_t...  5.54 us
    dynamic_slice x12, local copies, waits for them, and re-layouts, on_device(): lax.scan(absorb_block, (fresh_state(), fresh_state()), (block_list, jnp.a...  5.37 us
    dynamic_slice x4, local copies, waits for them, and re-layouts, absorb_block(): key_positions = lax.dynamic_slice_in_dim(positions, first_row, local_rows)  3 us
    le x4, local copies, waits for them, and re-layouts, absorb_block(): key_positions[None, :] <= own_positions[half_index][:, None]  2.99 us
  transfers between devices with their start and end apart: 3, of which 3 were waited for; matrix products, arithmetic and copies ran while one was open for 7% of the time, Pallas kernels for 0%

commit v1 on v0

--- a/solution.py
+++ b/solution.py
@@ -10,6 +10,16 @@
 NDOC = 8
 QUERIES_PER_KV = 8
 MASK_FLOOR = -1e30
+
+
+def around_the_ring(x, name, dim):
+    size = lax.axis_size(name)
+    held, shards = (x, [x])
+    for _ in range(size - 1):
+        held = lax.ppermute(held, name, [(i, (i + 1) % size) for i in range(size)])
+        shards.insert(0, held)
+    flat = jnp.concatenate(shards, axis=dim)
+    return jnp.roll(flat, (lax.axis_index(name) + 1) * x.shape[dim], axis=dim)
 
 
 def passed_along(array, axis, by):
@@ -96,7 +106,7 @@
             jnp.zeros((KEY_VALUE_HEADS, QUERIES_PER_KV * exchanged_rows, HEAD_SIZE), jnp.float32),
         )
 
-    portion = lax.all_gather(key_values, "ctx", axis=0, tiled=True)
+    portion = around_the_ring(key_values, "ctx", 0)
     piece_rows = portion.shape[0]
     count_of_blocks = piece_rows // local_rows
     block_list = portion.reshape(count_of_blocks, local_rows, 2, KEY_VALUE_HEADS, HEAD_SIZE)

time: 126 us -> 111 us (0.88)
  between operations: 13.5 us -> 0.22 us
  waiting for transfers between devices: 47.9 us -> 42.9 us
  starting transfers between devices: 2.68 us -> 5.31 us
  local copies, waits for them, and re-layouts: 28.8 us -> 27 us
    all_gather x1 -> x0, waiting for transfers between devices: 20.3 us -> none  [on_device(): portion = lax.all_gather(key_values, 'ctx', axis=0, tiled=True)]
    ppermute x0 -> x3, waiting for transfers between devices: none -> 15.8 us  [around_the_ring(): held = lax.ppermute(held, name, [(i, (i + 1) % size) for i in range(size)])]
    ppermute x0 -> x3, starting transfers between devices: none -> 2.63 us  [around_the_ring(): held = lax.ppermute(held, name, [(i, (i + 1) % size) for i in range(size)])]
  transfers between devices with their start and end apart: 3 -> 5, of which waited for: 3 -> 5; matrix products, arithmetic and copies ran while one was open for 7% -> 10% of each run, Pallas kernels for 0% -> 0%
where the time goes in v1:
time: 111 us; the launch traced here: 109 us
  waiting for transfers between devices  42.9 us (39%)
  local copies, waits for them, and re-layouts  27 us (24%)
  other arithmetic  17.4 us (16%)
  matrix products  8.42 us (8%)
  loops' own time  8.01 us (7%)
  starting transfers between devices  5.31 us (5%)
    ppermute x2, waiting for transfers between devices, passed_along(): lax.ppermute(array, axis, [(i, (i + by) % devices) for i in range(devices)])  27.1 us
    ppermute x3, waiting for transfers between devices, around_the_ring(): held = lax.ppermute(held, name, [(i, (i + 1) % size) for i in range(size)])  15.8 us
    another operation x1, loops' own time, on_device(): lax.scan(absorb_block, (fresh_state(), fresh_state()), (block_list, jnp.a...  7.69 us
    reduce_or x4, other arithmetic, absorb_block(): jnp.any(visible)  5.57 us
    dot_general x4, matrix products, attend(): jnp.einsum('hqd,khd->hqk', query_head_rows, key_rows, preferred_element_t...  5.55 us
    dynamic_slice x12, local copies, waits for them, and re-layouts, on_device(): lax.scan(absorb_block, (fresh_state(), fresh_state()), (block_list, jnp.a...  5.22 us
    le x4, local copies, waits for them, and re-layouts, absorb_block(): key_positions[None, :] <= own_positions[half_index][:, None]  3.05 us
    dynamic_slice x4, local copies, waits for them, and re-layouts, absorb_block(): key_documents = lax.dynamic_slice_in_dim(documents, first_row, local_rows)  2.95 us
  transfers between devices with their start and end apart: 5, of which 5 were waited for; matrix products, arithmetic and copies ran while one was open for 10% of the time, Pallas kernels for 0%

profile of v1, /device:TPU:1, one launch (start us, length us, event | category | flops | bytes accessed | tf_op | source)
XLA Modules:
  0.0 109.2 jit_solution(6835966499299586308)
XLA Ops:
  0.0 2.7 %collective-permute-start = (bf16[128,5120]{1,0:T(8,128)(2,1)}, bf16[128,5120]{1,0:T(8,128)(2,1)S(1)}, u32[]{:S(2)}, u32[]{:S(2)}) collective-permute-start(bf16[128,5120]{1,0:T(8,128)(2,1)} %bitcast.102), channel_id=1, source_target_pairs={{0,4},{4,8},{8,12},{12,16},{16,20},{20,24},{24,28},{28,0},{1,5},{5... | collective-permute-start | bytes 3932168 | tf_op jit(solution)/shard_map/ppermute | solution.py:27
  2.7 0.7 compare_bitcast_fusion.1
  6.4 23.1 %collective-permute-done = bf16[128,5120]{1,0:T(8,128)(2,1)S(1)} collective-permute-done((bf16[128,5120]{1,0:T(8,128)(2,1)}, bf16[128,5120]{1,0:T(8,128)(2,1)S(1)}, u32[]{:S(2)}, u32[]{:S(2)}) %collective-permute-start) | collective-permute-done | bytes 1310752 | tf_op jit(solution)/shard_map/ppermute | solution.py:27
  29.5 4.0 %collective-permute-done.1 = bf16[128,5120]{1,0:T(8,128)(2,1)} collective-permute-done((bf16[128,5120]{1,0:T(8,128)(2,1)}, bf16[128,5120]{1,0:T(8,128)(2,1)}, u32[]{:S(2)}, u32[]{:S(2)}) %collective-permute-start.1) | collective-permute-done | bytes 1310752 | tf_op jit(solution)/shard_map/ppermute | solution.py:27
  33.5 2.0 %select_select_fusion = bf16[128,5120]{1,0:T(8,128)(2,1)S(1)} fusion(bf16[128,5120]{1,0:T(8,128)(2,1)S(1)} %collective-permute-done, bf16[128,5120]{1,0:T(8,128)(2,1)} %collective-permute-done.1, pred[128]{0:T(512)(128)(4,1)S(1)} %eq.77, pred[128]{0:T(512)(128)(4,1)S(1)} %eq.73, bf16[1,128,5120]{2,1,0:T(8,128)(2,1)} %param.10), kind=kLoop, calls=%fused_computation.43 | loop fusion | flops 1310720 | bytes 5243136 | tf_op jit(solution)/shard_map/jit(_where)/select_n | solution.py:82
  35.5 1.8 %collective-permute-start.2 = (bf16[128,1024]{1,0:T(8,128)(2,1)S(1)}, bf16[128,1024]{1,0:T(8,128)(2,1)S(1)}, u32[]{:S(2)}, u32[]{:S(2)}) collective-permute-start(bf16[128,1024]{1,0:T(8,128)(2,1)S(1)} %slice.38), channel_id=1, source_target_pairs={{0,1},{1,2},{2,3},{3,0},{4,5},{5,6},{6,7},{7,4},{8,9},{9,10},{10,1... | collective-permute-start | bytes 786440 | tf_op jit(solution)/shard_map/ppermute | solution.py:19
  38.1 5.4 %collective-permute-done.2 = bf16[128,1024]{1,0:T(8,128)(2,1)S(1)} collective-permute-done((bf16[128,1024]{1,0:T(8,128)(2,1)S(1)}, bf16[128,1024]{1,0:T(8,128)(2,1)S(1)}, u32[]{:S(2)}, u32[]{:S(2)}) %collective-permute-start.2) | collective-permute-done | bytes 262176 | tf_op jit(solution)/shard_map/ppermute | solution.py:19
  43.5 0.8 collective-permute-start.3
  45.7 0.7 dynamic_slice.27
  47.1 0.7 dynamic_slice.28
  48.5 3.9 %collective-permute-done.3 = bf16[128,1024]{1,0:T(8,128)(2,1)S(1)} collective-permute-done((bf16[128,1024]{1,0:T(8,128)(2,1)S(1)}, bf16[128,1024]{1,0:T(8,128)(2,1)S(1)}, u32[]{:S(2)}, u32[]{:S(2)}) %collective-permute-start.3) | collective-permute-done | bytes 262176 | tf_op jit(solution)/shard_map/ppermute | solution.py:19
  52.8 1.4 %copy.22 = bf16[2,64,4,8,128]{4,1,3,2,0:T(8,128)(2,1)} copy(bf16[2,64,4,8,128]{4,3,2,1,0:T(8,128)(2,1)S(1)} %bitcast.97) | data formatting | bytes 2097152 | tf_op jit(solution)/shard_map/reshape | solution.py:93
  54.2 6.6 %collective-permute-done.4 = bf16[128,1024]{1,0:T(8,128)(2,1)S(1)} collective-permute-done((bf16[128,1024]{1,0:T(8,128)(2,1)S(1)}, bf16[128,1024]{1,0:T(8,128)(2,1)S(1)}, u32[]{:S(2)}, u32[]{:S(2)}) %collective-permute-start.4) | collective-permute-done | bytes 262176 | tf_op jit(solution)/shard_map/ppermute | solution.py:19
  61.0 0.8 reshape.165
  63.7 41.9 %while.20 = (s32[]{:T(128)}, f32[4,512,1]{1,0,2:T(4,128)S(1)}, f32[4,512,1]{1,0,2:T(4,128)}, f32[4,512,128]{2,1,0:T(8,128)S(1)}, f32[4,512,1]{1,0,2:T(4,128)S(1)...) while((s32[]{:T(128)}, f32[4,512,1]{1,0,2:T(4,128)S(1)}, ...), condition=%wide.region_13.14_spmd, body=%wide.region_2.13_spmd.sunk | while | flops 274280448 | bytes 14785039 | solution.py:140
  63.7 1.2 %dynamic_slice.43 = s32[1]{0:T(128)} dynamic-slice(s32[4]{0:T(128)} %get-tuple-element.402, s32[]{:T(128)} %get-tuple-element.377), dynamic_slice_sizes={1} | dynamic-slice | bytes 12 | tf_op jit(solution)/shard_map/while/body/jit(dynamic_index_in_dim)/dynamic_slice | solution.py:140
  65.4 0.7 dynamic_slice.44
  66.1 0.7 dynamic_slice.45
  66.9 0.8 slice_bitcast_fusion.9
  67.6 1.4 %fusion.32 = (pred[]{:T(512)}, pred[64,128]{1,0:T(8,128)(4,1)S(1)}, pred[]{:T(512)}, pred[64,128]{1,0:T(8,128)(4,1)}) fusion(s32[64]{0:T(128)S(1)} %get-tuple-element.331, s32[128]{0:T(128)S(1)} %dynamic_slice.44, s32[64]{0:T(128)S(1)} %get-tuple-element.332, s32[128]{0:T(128)S(1)} %dynamic_slice.45, s32[64]{0:T(128)S(1)} %get-tuple-element.333, ...), kind=kLoop, calls=%fused_computation.73.clone.1 | loop fusion | flops 65534 | bytes 18434 | tf_op jit(solution)/shard_map/while/body/eval_jaxpr/reduce_or | solution.py:128
  69.8 3.9 %conditional.5 = ((f32[4,512,1]{1,0,2:T(4,128)S(1)}, f32[4,512,1]{1,0,2:T(4,128)}, f32[4,512,128]{2,1,0:T(8,128)S(1)})) conditional(s32[]{:T(128)} %convert_element_type.33, (f32[4,512,1]{1,0,2:T(4,128)S(1)}, f32[4,512,1]{1,0,2:T(4,128)}, f32[4,512,128]{2,1,0:T(8,128)S(1)}) %tuple.61, (pred[64,128]{1,0:T(8,128)(4,1)S(1)}, ...), branch_computations={%region_9.9_spmd, %region_10.12_spmd} | conditional | flops 137107456 | bytes 6561824 | solution.py:127
  70.0 1.4 %fusion.26 = (f32[4,512]{1,0:T(4,128)S(1)}, f32[4,512,128]{1,2,0:T(8,128)S(1)}) fusion(bf16[128,4,128]{2,0,1:T(8,128)(2,1)S(1)} %get-tuple-element.115, bf16[2,4,512,128]{3,2,1,0:T(8,128)(2,1)} %get-tuple-element.114, pred[512,128]{0,1:T(8,128)(4,1)S(1)} %copy.20), kind=kOutput, calls=%fused_computation.76 | convolution fusion | flops 67893248 | bytes 1777664 | tf_op jit(solution)/shard_map/while/body/eval_jaxpr/cond/branch_1_fun/hqd,khd->hqk/dot_general | solution.py:46
  71.7 1.3 %bitcast_add_fusion.1 = f32[4,512,1]{1,0,2:T(4,128)} fusion(f32[4,512]{1,0:T(4,128)S(1)} %fusion.13, f32[4,512,1]{1,0,2:T(4,128)} %get-tuple-element.116, f32[4,512,1]{1,0,2:T(4,128)S(1)} %get-tuple-element.112, f32[4,512,1]{1,0,2:T(4,128)S(1)} %get-tuple-element.356), kind=kLoop, calls=%fused_computation.28 | loop fusion | flops 6144 | bytes 40960 | tf_op jit(solution)/shard_map/while/body/eval_jaxpr/cond/branch_1_fun/add | solution.py:54
  74.4 3.3 %conditional.4 = ((f32[4,512,1]{1,0,2:T(4,128)S(1)}, f32[4,512,1]{1,0,2:T(4,128)}, f32[4,512,128]{2,1,0:T(8,128)S(1)})) conditional(s32[]{:T(128)} %convert_element_type.32, (f32[4,512,1]{1,0,2:T(4,128)S(1)}, f32[4,512,1]{1,0,2:T(4,128)}, f32[4,512,128]{2,1,0:T(8,128)S(1)}) %tuple.59, (pred[64,128]{1,0:T(8,128)(4,1)}, ...), branch_computations={%region_4.4_spmd, %region_5.7_spmd} | conditional | flops 137107456 | bytes 6627416 | solution.py:127
  75.3 1.4 %fusion.25 = (f32[4,512]{1,0:T(4,128)S(1)}, f32[4,512,128]{1,2,0:T(8,128)S(1)}) fusion(bf16[128,4,128]{2,0,1:T(8,128)(2,1)S(1)} %get-tuple-element.108, bf16[2,4,512,128]{3,2,1,0:T(8,128)(2,1)} %get-tuple-element.107, pred[512,128]{0,1:T(8,128)(4,1)S(1)} %copy.18), kind=kOutput, calls=%fused_computation.75 | convolution fusion | flops 67893248 | bytes 1777664 | tf_op jit(solution)/shard_map/while/body/eval_jaxpr/cond/branch_1_fun/hqd,khd->hqk/dot_general | solution.py:46
  77.7 1.2 %dynamic_slice.43 = s32[1]{0:T(128)} dynamic-slice(s32[4]{0:T(128)} %get-tuple-element.402, s32[]{:T(128)} %get-tuple-element.377), dynamic_slice_sizes={1} | dynamic-slice | bytes 12 | tf_op jit(solution)/shard_map/while/body/jit(dynamic_index_in_dim)/dynamic_slice | solution.py:140
  79.5 0.7 dynamic_slice.44
  80.2 0.7 dynamic_slice.45
  81.0 0.8 slice_bitcast_fusion.9
  81.7 1.4 %fusion.32 = (pred[]{:T(512)}, pred[64,128]{1,0:T(8,128)(4,1)S(1)}, pred[]{:T(512)}, pred[64,128]{1,0:T(8,128)(4,1)}) fusion(s32[64]{0:T(128)S(1)} %get-tuple-element.331, s32[128]{0:T(128)S(1)} %dynamic_slice.44, s32[64]{0:T(128)S(1)} %get-tuple-element.332, s32[128]{0:T(128)S(1)} %dynamic_slice.45, s32[64]{0:T(128)S(1)} %get-tuple-element.333, ...), kind=kLoop, calls=%fused_computation.73.clone.1 | loop fusion | flops 65534 | bytes 18434 | tf_op jit(solution)/shard_map/while/body/eval_jaxpr/reduce_or | solution.py:128
  84.6 3.3 %conditional.4 = ((f32[4,512,1]{1,0,2:T(4,128)S(1)}, f32[4,512,1]{1,0,2:T(4,128)}, f32[4,512,128]{2,1,0:T(8,128)S(1)})) conditional(s32[]{:T(128)} %convert_element_type.32, (f32[4,512,1]{1,0,2:T(4,128)S(1)}, f32[4,512,1]{1,0,2:T(4,128)}, f32[4,512,128]{2,1,0:T(8,128)S(1)}) %tuple.59, (pred[64,128]{1,0:T(8,128)(4,1)}, ...), branch_computations={%region_4.4_spmd, %region_5.7_spmd} | conditional | flops 137107456 | bytes 6627416 | solution.py:127
  85.5 1.4 %fusion.25 = (f32[4,512]{1,0:T(4,128)S(1)}, f32[4,512,128]{1,2,0:T(8,128)S(1)}) fusion(bf16[128,4,128]{2,0,1:T(8,128)(2,1)S(1)} %get-tuple-element.108, bf16[2,4,512,128]{3,2,1,0:T(8,128)(2,1)} %get-tuple-element.107, pred[512,128]{0,1:T(8,128)(4,1)S(1)} %copy.18), kind=kOutput, calls=%fused_computation.75 | convolution fusion | flops 67893248 | bytes 1777664 | tf_op jit(solution)/shard_map/while/body/eval_jaxpr/cond/branch_1_fun/hqd,khd->hqk/dot_general | solution.py:46
  87.2 0.7 convolution_add_fusion
  88.0 1.2 %dynamic_slice.43 = s32[1]{0:T(128)} dynamic-slice(s32[4]{0:T(128)} %get-tuple-element.402, s32[]{:T(128)} %get-tuple-element.377), dynamic_slice_sizes={1} | dynamic-slice | bytes 12 | tf_op jit(solution)/shard_map/while/body/jit(dynamic_index_in_dim)/dynamic_slice | solution.py:140
  89.7 0.7 dynamic_slice.44
  90.4 0.7 dynamic_slice.45
  91.2 0.8 slice_bitcast_fusion.9
  91.9 1.4 %fusion.32 = (pred[]{:T(512)}, pred[64,128]{1,0:T(8,128)(4,1)S(1)}, pred[]{:T(512)}, pred[64,128]{1,0:T(8,128)(4,1)}) fusion(s32[64]{0:T(128)S(1)} %get-tuple-element.331, s32[128]{0:T(128)S(1)} %dynamic_slice.44, s32[64]{0:T(128)S(1)} %get-tuple-element.332, s32[128]{0:T(128)S(1)} %dynamic_slice.45, s32[64]{0:T(128)S(1)} %get-tuple-element.333, ...), kind=kLoop, calls=%fused_computation.73.clone.1 | loop fusion | flops 65534 | bytes 18434 | tf_op jit(solution)/shard_map/while/body/eval_jaxpr/reduce_or | solution.py:128
  94.1 3.9 %conditional.5 = ((f32[4,512,1]{1,0,2:T(4,128)S(1)}, f32[4,512,1]{1,0,2:T(4,128)}, f32[4,512,128]{2,1,0:T(8,128)S(1)})) conditional(s32[]{:T(128)} %convert_element_type.33, (f32[4,512,1]{1,0,2:T(4,128)S(1)}, f32[4,512,1]{1,0,2:T(4,128)}, f32[4,512,128]{2,1,0:T(8,128)S(1)}) %tuple.61, (pred[64,128]{1,0:T(8,128)(4,1)S(1)}, ...), branch_computations={%region_9.9_spmd, %region_10.12_spmd} | conditional | flops 137107456 | bytes 6561824 | solution.py:127
  94.3 1.4 %fusion.26 = (f32[4,512]{1,0:T(4,128)S(1)}, f32[4,512,128]{1,2,0:T(8,128)S(1)}) fusion(bf16[128,4,128]{2,0,1:T(8,128)(2,1)S(1)} %get-tuple-element.115, bf16[2,4,512,128]{3,2,1,0:T(8,128)(2,1)} %get-tuple-element.114, pred[512,128]{0,1:T(8,128)(4,1)S(1)} %copy.20), kind=kOutput, calls=%fused_computation.76 | convolution fusion | flops 67893248 | bytes 1777664 | tf_op jit(solution)/shard_map/while/body/eval_jaxpr/cond/branch_1_fun/hqd,khd->hqk/dot_general | solution.py:46
  96.0 1.3 %bitcast_add_fusion.1 = f32[4,512,1]{1,0,2:T(4,128)} fusion(f32[4,512]{1,0:T(4,128)S(1)} %fusion.13, f32[4,512,1]{1,0,2:T(4,128)} %get-tuple-element.116, f32[4,512,1]{1,0,2:T(4,128)S(1)} %get-tuple-element.112, f32[4,512,1]{1,0,2:T(4,128)S(1)} %get-tuple-element.356), kind=kLoop, calls=%fused_computation.28 | loop fusion | flops 6144 | bytes 40960 | tf_op jit(solution)/shard_map/while/body/eval_jaxpr/cond/branch_1_fun/add | solution.py:54
  98.7 1.2 %dynamic_slice.43 = s32[1]{0:T(128)} dynamic-slice(s32[4]{0:T(128)} %get-tuple-element.402, s32[]{:T(128)} %get-tuple-element.377), dynamic_slice_sizes={1} | dynamic-slice | bytes 12 | tf_op jit(solution)/shard_map/while/body/jit(dynamic_index_in_dim)/dynamic_slice | solution.py:140
  100.5 0.7 dynamic_slice.44
  101.2 0.7 dynamic_slice.45
  101.9 0.8 slice_bitcast_fusion.9
  102.7 1.4 %fusion.32 = (pred[]{:T(512)}, pred[64,128]{1,0:T(8,128)(4,1)S(1)}, pred[]{:T(512)}, pred[64,128]{1,0:T(8,128)(4,1)}) fusion(s32[64]{0:T(128)S(1)} %get-tuple-element.331, s32[128]{0:T(128)S(1)} %dynamic_slice.44, s32[64]{0:T(128)S(1)} %get-tuple-element.332, s32[128]{0:T(128)S(1)} %dynamic_slice.45, s32[64]{0:T(128)S(1)} %get-tuple-element.333, ...), kind=kLoop, calls=%fused_computation.73.clone.1 | loop fusion | flops 65534 | bytes 18434 | tf_op jit(solution)/shard_map/while/body/eval_jaxpr/reduce_or | solution.py:128
  105.6 1.4 %divide_convert_fusion = (bf16[4,512,128]{2,1,0:T(8,128)(2,1)S(1)}, bf16[4,512,128]{2,1,0:T(8,128)(2,1)S(1)}) fusion(f32[4,512,128]{2,1,0:T(8,128)S(1)} %get-tuple-element.146, f32[4,512]{1,0:T(4,128)} %bitcast.31, f32[4,512,128]{2,1,0:T(8,128)S(1)} %get-tuple-element.144, f32[4,512]{1,0:T(4,128)} %bitcast.105), kind=kLoop, calls=%fused_computation.46 | loop fusion | flops 1048576 | bytes 3162112 | tf_op jit(solution)/shard_map/convert.4
  108.2 1.0 pad_maximum_fusion
  (95 shorter events, 16.1 us)
Async XLA Ops:
  0.0 29.5 %collective-permute-start = (bf16[128,5120]{1,0:T(8,128)(2,1)}, bf16[128,5120]{1,0:T(8,128)(2,1)S(1)}, u32[]{:S(2)}, u32[]{:S(2)}) collective-permute-start(bf16[128,5120]{1,0:T(8,128)(2,1)} %bitcast.102), channel_id=1, source_target_pairs={{0,4},{4,8},{8,12},{12,16},{16,20},{20,24},{24,28},{28,0},{1,5},{5... | collective-permute-start | bytes 3932168 | tf_op jit(solution)/shard_map/ppermute | solution.py:27
  2.7 30.8 %collective-permute-start.1 = (bf16[128,5120]{1,0:T(8,128)(2,1)}, bf16[128,5120]{1,0:T(8,128)(2,1)}, u32[]{:S(2)}, u32[]{:S(2)}) collective-permute-start(bf16[128,5120]{1,0:T(8,128)(2,1)} %bitcast.103), channel_id=1, source_target_pairs={{0,28},{4,0},{8,4},{12,8},{16,12},{20,16},{24,20},{28,24},{1,29},{... | collective-permute-start | bytes 3932168 | tf_op jit(solution)/shard_map/ppermute | solution.py:27
  6.4 30.8 %copy-start.2 = (s32[8,8]{1,0:T(8,128)S(1)}, s32[8,8]{1,0:T(8,128)}, u32[]{:S(2)}) copy-start(s32[8,8]{1,0:T(8,128)} %param.13) | copy-start | bytes 772
  35.5 8.0 %collective-permute-start.2 = (bf16[128,1024]{1,0:T(8,128)(2,1)S(1)}, bf16[128,1024]{1,0:T(8,128)(2,1)S(1)}, u32[]{:S(2)}, u32[]{:S(2)}) collective-permute-start(bf16[128,1024]{1,0:T(8,128)(2,1)S(1)} %slice.38), channel_id=1, source_target_pairs={{0,1},{1,2},{2,3},{3,0},{4,5},{5,6},{6,7},{7,4},{8,9},{9,10},{10,1... | collective-permute-start | bytes 786440 | tf_op jit(solution)/shard_map/ppermute | solution.py:19
  43.5 8.9 %collective-permute-start.3 = (bf16[128,1024]{1,0:T(8,128)(2,1)S(1)}, bf16[128,1024]{1,0:T(8,128)(2,1)S(1)}, u32[]{:S(2)}, u32[]{:S(2)}) collective-permute-start(bf16[128,1024]{1,0:T(8,128)(2,1)S(1)} %collective-permute-done.2), channel_id=1, source_target_pairs={{0,1},{1,2},{2,3},{3,0},{4,5},{5,6},{6,7},{7,4},{8,9},{9,10},{10,1... | collective-permute-start | bytes 786440 | tf_op jit(solution)/shard_map/ppermute | solution.py:19
  52.4 8.4 %collective-permute-start.4 = (bf16[128,1024]{1,0:T(8,128)(2,1)S(1)}, bf16[128,1024]{1,0:T(8,128)(2,1)S(1)}, u32[]{:S(2)}, u32[]{:S(2)}) collective-permute-start(bf16[128,1024]{1,0:T(8,128)(2,1)S(1)} %collective-permute-done.3), channel_id=1, source_target_pairs={{0,1},{1,2},{2,3},{3,0},{4,5},{5,6},{6,7},{7,4},{8,9},{9,10},{10,1... | collective-permute-start | bytes 786440 | tf_op jit(solution)/shard_map/ppermute | solution.py:19
  75.3 1.6 %copy-start = (f32[4,512,1]{1,0,2:T(4,128)S(1)}, f32[4,512,1]{1,0,2:T(4,128)}, u32[]{:S(2)}) copy-start(f32[4,512,1]{1,0,2:T(4,128)} %get-tuple-element.109) | copy-start | bytes 24580 | tf_op jit(solution)/shard_map/while/body/eval_jaxpr/cond
  76.9 0.8 copy-start.1
  85.5 1.7 %copy-start = (f32[4,512,1]{1,0,2:T(4,128)S(1)}, f32[4,512,1]{1,0,2:T(4,128)}, u32[]{:S(2)}) copy-start(f32[4,512,1]{1,0,2:T(4,128)} %get-tuple-element.109) | copy-start | bytes 24580 | tf_op jit(solution)/shard_map/while/body/eval_jaxpr/cond
  87.2 0.8 copy-start.1
